TPU v7x, 128 devices: a whole 4x4x4 slice. The times are simulated.
128 devices in a mesh: row: 4 (over z), col: 32 (over x, y, core).
Axes of the slice: x: 4, y: 4, z: 4, core: 2. Of those that a mesh axis runs over, the one named last changes fastest.
Arguments:
- neighbor: int32 [32, 3072, 3072], P(None, 'col', 'row'), may hold values from 0 to 1, as said below
- true_coords: float32 [32, 3, 3072], P(None, None, ('row', 'col')), as said below
- pred_coords: float32 [32, 3, 3072], P(None, None, ('row', 'col')), as said below
- residue_mask: int32 [32, 3072], P(None, ('row', 'col')), may hold values from 0 to 1, as said below
- single: bfloat16 [32, 3072, 384], P(None, ('row', 'col'))
- ln_gain: float32 [384], replicated, may hold values from 0.1 to 1.9
- w_hidden: bfloat16 [384, 128], replicated, may hold values from -0.3125 to 0.3125
- b_hidden: float32 [128], replicated, may hold values from -3 to 3
- w_mid: bfloat16 [128, 128], replicated, may hold values from -0.5 to 0.5
- b_mid: float32 [128], replicated, may hold values from -3 to 3
- w_logits: bfloat16 [128, 50], replicated, may hold values from -1.5 to 1.5
- b_logits: float32 [50], replicated, may hold values from -4 to 4
Outputs:
- lddt_score: float32 [32, 3072], P(None, ('row', 'col'))
- residue_loss: float32 [32, 3072], P(None, ('row', 'col'))
- total_loss: float32 [], replicated
Inputs may be any that keep to these rules, and one draw needn't show every extreme that they name: `neighbor`: 0 or 1; 0 where j == i; 1 wherever 0 < |i - j| <= 8. `residue_mask`: per structure, 1 on a leading run of 1536 or more residues and 0 after it. `true_coords`: positions in angstroms. `pred_coords`: positions in angstroms.
All inputs are finite; a program needn't handle non-finite values.
Results may differ from a plain program's by a relative error of at most 0.00098.
Values sent between devices are 32-bit elements; how exact they have to be, the bound alone decides.
A program may use at most 64 MiB of HBM per device.

v0:
```python
import jax
import jax.numpy as jnp
from jax import lax
from jax.sharding import Mesh
from jax.sharding import PartitionSpec as P

L = 3072
COL = ("col_0", "col_1", "col_2")
ROW_COL = ("row", "col_0", "col_1", "col_2")
THRESHOLDS = (0.5, 1.0, 2.0, 4.0)


def in_order(parts, dim):
    parts = jnp.moveaxis(parts, 0, dim)
    lengths = parts.shape
    return parts.reshape(*lengths[:dim], lengths[dim] * lengths[dim + 1], *lengths[dim + 2 :])


def sent_to_all(shard, axis):
    copies = jnp.broadcast_to(shard, (lax.axis_size(axis), *shard.shape))
    return lax.all_to_all(copies, axis, split_axis=0, concat_axis=0, tiled=True)


def gather_directly(shard, axis, dim):
    return in_order(sent_to_all(shard, axis), dim)


def from_root(shard, axis, root):
    return lax.dynamic_index_in_dim(lax.all_gather(shard, axis), root, 0, keepdims=False)


def split_up(shard, dim, size):
    before, after = (shard.shape[:dim], shard.shape[dim + 1 :])
    return jnp.moveaxis(shard.reshape(*before, size, -1, *after), dim, 0)


def summed_on_arrival(shard, axis, dim):
    size = lax.axis_size(axis)
    parts = lax.all_to_all(split_up(shard, dim, size), axis, 0, 0, tiled=True)
    return jnp.sum(parts, axis=0)


def sent_together(arrays, axis, dim, along):
    ends, at = ([], 0)
    for a in arrays[:-1]:
        at += a.shape[along]
        ends.append(at)
    both = jnp.concatenate(arrays, axis=along)
    return tuple(jnp.split(summed_on_arrival(both, axis, dim), ends, axis=along))


def over_axes(shard, axes):
    for axis in axes:
        shard = lax.psum(shard, axis)
    return shard


def tile_dist(rows_block, cols_block):
    total = (cols_block[:, 0, :, None] - rows_block[:, 0, None, :]) ** 2
    total = total + (cols_block[:, 1, :, None] - rows_block[:, 1, None, :]) ** 2
    total = total + (cols_block[:, 2, :, None] - rows_block[:, 2, None, :]) ** 2
    return jnp.sqrt(total + 1e-10)


def head_loss(lddt_value, single, ln_gain, w_hidden, b_hidden, w_mid, b_mid, w_logits, b_logits):
    features = single.astype(jnp.float32)
    average = jnp.mean(features, axis=-1, keepdims=True)
    centred = features - average
    variance = jnp.mean(centred * centred, axis=-1, keepdims=True)
    normed = (centred * lax.rsqrt(variance + 1e-05) * ln_gain).astype(jnp.bfloat16)
    first_hidden = jax.nn.relu(
        jnp.dot(normed, w_hidden, preferred_element_type=jnp.float32) + b_hidden
    ).astype(jnp.bfloat16)
    second_hidden = jax.nn.relu(
        jnp.dot(first_hidden, w_mid, preferred_element_type=jnp.float32) + b_mid
    ).astype(jnp.bfloat16)
    logits = jnp.dot(second_hidden, w_logits, preferred_element_type=jnp.float32) + b_logits
    log_total = jnp.log(jnp.sum(jnp.exp(logits), axis=-1))
    bins = logits.shape[-1]
    centers = (jnp.arange(bins).astype(jnp.float32) + 0.5) / bins
    closeness = jnp.exp(-((lddt_value[..., None] - centers) ** 2) * (bins * bins * 0.5))
    target = closeness / jnp.sum(closeness, axis=-1, keepdims=True)
    return log_total - jnp.sum(target * logits, axis=-1)


def local(
    neighbor,
    true_coords,
    pred_coords,
    residue_mask,
    single,
    ln_gain,
    w_hidden,
    b_hidden,
    w_mid,
    b_mid,
    w_logits,
    b_logits,
):
    valid = residue_mask.astype(jnp.float32)
    stacked = jnp.concatenate([true_coords, pred_coords, valid[:, None, :]], axis=1)
    row_count = lax.axis_size("row")
    col_count = lax.axis_size(COL)
    rows_len = L // row_count
    cols_len = L // col_count
    col_index = lax.axis_index(COL)
    rows_part = gather_directly(stacked, COL, 2)
    offset = col_index * cols_len % rows_len
    column_piece = lax.dynamic_slice_in_dim(rows_part, offset, cols_len, 2)
    source_row = col_index * cols_len // rows_len
    cols_part = from_root(column_piece, "row", source_row)
    true_dist = tile_dist(rows_part[:, 0:3], cols_part[:, 0:3])
    pred_dist = tile_dist(rows_part[:, 3:6], cols_part[:, 3:6])
    mismatch = jnp.abs(pred_dist - true_dist)
    scores = jnp.zeros_like(mismatch)
    for threshold in THRESHOLDS:
        scores = scores + jax.nn.sigmoid(4.0 * (threshold - mismatch))
    scores = 0.25 * scores
    weights = neighbor.astype(jnp.float32) * rows_part[:, 6, None, :] * cols_part[:, 6, :, None]
    preserved = jnp.sum(weights * scores, axis=1)
    neighbors = jnp.sum(weights, axis=1)
    preserved_own, neighbors_own = sent_together((preserved, neighbors), COL, 1, 0)
    lddt_score = preserved_own / jnp.maximum(neighbors_own, 1.0)
    residue_loss = valid * head_loss(
        lddt_score, single, ln_gain, w_hidden, b_hidden, w_mid, b_mid, w_logits, b_logits
    )
    loss_sum, valid_sum = (
        over_axes(jnp.sum(residue_loss), ROW_COL),
        over_axes(jnp.sum(valid), ROW_COL),
    )
    total_loss = loss_sum / valid_sum
    return (lddt_score, residue_loss, total_loss)


def solution(mesh):
    torus = Mesh(
        mesh.devices.reshape(mesh.shape["row"], 4, 4, 2), ("row", "col_0", "col_1", "col_2")
    )
    placed = (
        P(None, COL, "row"),
        P(None, None, ROW_COL),
        P(None, None, ROW_COL),
        P(None, ROW_COL),
        P(None, ROW_COL, None),
        P(),
        P(),
        P(),
        P(),
        P(),
        P(),
        P(),
    )
    return jax.shard_map(
        local,
        mesh=torus,
        in_specs=placed,
        out_specs=(P(None, ROW_COL), P(None, ROW_COL), P()),
        check_vma=False,
    )
```

profile of v0, /device:TPU:1, one launch (start us, length us, event | category | flops | bytes accessed | tf_op | source)
XLA Modules:
  0.0 134.1 jit_solution(17454920612350802530)
XLA Ops:
  0.6 0.0 copy-start
  0.6 0.8 copy.19
  1.5 0.1 copy.20
  1.5 0.8 pad_maximum_fusion.1
  2.3 0.2 broadcast_bitcast_fusion
  2.5 2.1 %reshape.49 = f32[32,1,5376]{2,1,0:T(1,128)} reshape(f32[32,7,24,32]{3,2,1,0:T(8,128)S(1)} %broadcast_bitcast_fusion) | data formatting | bytes 1376256
  4.6 8.6 %all-to-all-start = ((f32[32,1,5376]{2,1,0:T(1,128)}), f32[32,1,5376]{2,1,0:T(1,128)S(1)}, u32[]{:S(2)}, u32[]{:S(2)}) async-start(f32[32,1,5376]{2,1,0:T(1,128)} %reshape.49), calls=%async_computation | async-start | bytes 1376256 | tf_op jit(solution)/shard_map/all_to_all | solution.py:21
  13.2 1.2 convert_reduce_fusion
  14.4 0.5 add_multiply_fusion
  15.0 1.4 %fusion.8 = f32[32,24]{1,0:T(8,128)S(1)} fusion(bf16[32,24,384]{2,1,0:T(8,128)(2,1)} %param.16, f32[32,24]{1,0:T(8,128)S(1)} %broadcast_multiply_fusion), kind=kLoop, calls=%fused_computation.15 | loop fusion | flops 1178880 | bytes 595968 | tf_op jit(solution)/shard_map/reduce_sum | solution.py:69
  16.4 0.0 copy-done
  16.4 2.6 %fusion.12 = bf16[32,24,128]{2,1,0:T(8,128)(2,1)} fusion(bf16[32,24,384]{2,1,0:T(8,128)(2,1)} %param.16, f32[384]{0:T(512)} %param.17, f32[32,24]{1,0:T(8,128)S(1)} %add_rsqrt_fusion, f32[32,24]{1,0:T(8,128)S(1)} %broadcast_multiply_fusion, f32[128]{0:T(128)} %param.21, f32[128]{0:T(128)} %param.19, bf16[384,128]{1,0:T(8,128)(2,1)S(1)} %copy-done, ...), kind=kOutput, calls=%fused_computation.19 | convolution fusion | flops 102727680 | bytes 926208 | tf_op jit(solution)/shard_map/dot_general | solution.py:75
  19.0 7.5 %all-to-all-done = f32[32,1,5376]{2,1,0:T(1,128)S(1)} async-done(((f32[32,1,5376]{2,1,0:T(1,128)}), f32[32,1,5376]{2,1,0:T(1,128)S(1)}, u32[]{:S(2)}, u32[]{:S(2)}) %all-to-all-start) | async-done | bytes 688160 | tf_op jit(solution)/shard_map/all_to_all | solution.py:21
  26.4 0.5 broadcast.53
  26.9 2.3 %reduce = f32[32,5376]{1,0:T(8,128)S(1)} reduce(f32[32,1,5376]{2,1,0:T(1,128)S(1)} %all-to-all-done, f32[]{:T(128)} %broadcast.53), dimensions={1}, to_apply=%all_to_all.6.reduce_sub_computation | reduce | bytes 1376260 | tf_op jit(solution)/shard_map/all_to_all | solution.py:21
  29.2 0.8 reshape.50
  30.0 1.7 %bitcast_bitcast_fusion = f32[32,7,32,24]{0,3,1,2:T(8,128)} fusion(f32[32,7,24,32]{3,2,1,0:T(8,128)S(1)} %reshape.50), kind=kLoop, calls=%fused_computation.64 | loop fusion | bytes 1376256 | tf_op jit(solution)/shard_map/transpose | solution.py:14
  31.7 5.6 %copy.21 = f32[32,7,32,24]{3,2,0,1:T(8,128)} copy(f32[32,7,32,24]{0,3,1,2:T(8,128)} %bitcast_bitcast_fusion) | data formatting | bytes 1376256 | tf_op jit(solution)/shard_map/transpose | solution.py:14
  37.3 3.6 %reshape.43 = f32[32,7,768]{2,0,1:T(8,128)S(1)} reshape(f32[32,7,32,24]{3,2,0,1:T(8,128)} %copy.21) | data formatting | bytes 1376256 | tf_op jit(solution)/shard_map/reshape | solution.py:16
  40.9 0.1 constant_dynamic-slice_fusion
  41.0 12.0 %all-gather = f32[128,7,96]{2,0,1:T(8,128)S(1)} all-gather(f32[32,7,96]{2,0,1:T(8,128)S(1)} %constant_dynamic-slice_fusion), channel_id=2, replica_groups=mesh['row'=4,'col_0'=4,'col_1'=4,'col_2'=2] {'row'}, dimensions={0}, use_global_device_ids=true | all-gather | bytes 430080 | tf_op jit(solution)/shard_map/all_gather | solution.py:29
  53.1 0.0 copy-start.1
  53.1 0.0 copy-start.3
  53.1 0.0 copy-start.4
  53.1 0.0 copy-start.5
  53.1 26.3 %multiply_reduce_fusion = (f32[32,768]{1,0:T(8,128)S(1)}, f32[32,768]{1,0:T(8,128)S(1)}) fusion(s32[32,96,768]{2,1,0:T(8,128)} %param.12, f32[32,768]{1,0:T(8,128)S(1)} %get-tuple-element.19, f32[32,96]{1,0:T(8,128)S(1)} %get-tuple-element.26, f32[32,768]{1,0:T(8,128)S(1)} %get-tuple-element.20, f32[32,96]{1,0:T(8,128)S(1)} %get-tuple-element.27, ...), kind=kLoop, calls=%fused_computation.1 | loop fusion | flops 117915648 | bytes 10407936 | tf_op jit(solution)/shard_map/reduce_sum | solution.py:120
  79.5 0.2 copy.22
  79.6 0.9 reshape.51
  80.6 5.6 %all-to-all-start.1 = ((f32[32,1,1536]{2,1,0:T(1,128)}), f32[32,1,1536]{2,1,0:T(1,128)S(1)}, u32[]{:S(2)}, u32[]{:S(2)}) async-start(f32[32,1,1536]{2,1,0:T(1,128)} %reshape.51), calls=%async_computation.1 | async-start | bytes 393216 | tf_op jit(solution)/shard_map/all_to_all | solution.py:39
  86.1 0.0 copy-done.1
  86.1 0.0 copy-done.3
  86.2 0.0 copy-done.4
  86.2 0.3 exponential_reduce_fusion
  86.5 8.0 %all-to-all-done.1 = f32[32,1,1536]{2,1,0:T(1,128)S(1)} async-done(((f32[32,1,1536]{2,1,0:T(1,128)}), f32[32,1,1536]{2,1,0:T(1,128)S(1)}, u32[]{:S(2)}, u32[]{:S(2)}) %all-to-all-start.1) | async-done | bytes 196640 | tf_op jit(solution)/shard_map/all_to_all | solution.py:39
  94.5 1.1 reduce.1
  95.6 0.1 reshape.52
  95.8 0.1 fusion.31
  95.8 0.0 copy-start.2
  95.9 0.1 copy.23
  95.9 0.0 copy-done.5
  95.9 0.6 fusion.35
  96.6 0.6 fusion.34
  97.2 0.7 copy.24
  97.8 9.7 %all-reduce.2 = (f32[]{:T(128)}, f32[]{:T(128)}) all-reduce(f32[]{:T(128)} %get-tuple-element.16, f32[]{:T(128)} %get-tuple-element.32), channel_id=1, replica_groups=mesh['row'=4,'col_0'=4,'col_1'=4,'col_2'=2] {'row'}, use_global_device_ids=true, to_apply=%region_9.10 | all-reduce | flops 2 | bytes 16 | tf_op jit(solution)/shard_map/psum | solution.py:54
  107.6 7.4 %all-reduce.1 = (f32[]{:T(128)}, f32[]{:T(128)}) all-reduce(f32[]{:T(128)} %get-tuple-element.12, f32[]{:T(128)} %get-tuple-element.13), channel_id=1, replica_groups=mesh['row'=4,'col_0'=4,'col_1'=4,'col_2'=2] {'col_0'}, use_global_device_ids=true, to_apply=%region_10.11 | all-reduce | flops 2 | bytes 16 | tf_op jit(solution)/shard_map/psum | solution.py:54
  115.0 7.7 %all-reduce = (f32[]{:T(128)}, f32[]{:T(128)}) all-reduce(f32[]{:T(128)} %get-tuple-element.10, f32[]{:T(128)} %get-tuple-element.11), channel_id=1, replica_groups=mesh['row'=4,'col_0'=4,'col_1'=4,'col_2'=2] {'col_1'}, use_global_device_ids=true, to_apply=%region_11.12 | all-reduce | flops 2 | bytes 16 | tf_op jit(solution)/shard_map/psum | solution.py:54
  122.7 9.1 %all-reduce.3 = (f32[]{:T(128)}, f32[]{:T(128)}) all-reduce(f32[]{:T(128)} %get-tuple-element.8, f32[]{:T(128)} %get-tuple-element.9), channel_id=1, replica_groups=mesh['row'=4,'col_0'=4,'col_1'=4,'col_2'=2] {'col_2'}, use_global_device_ids=true, to_apply=%region_12.13 | all-reduce | flops 2 | bytes 16 | tf_op jit(solution)/shard_map/psum | solution.py:54
  133.0 0.0 copy-done.2
  (8 shorter events, 0.1 us)
Async XLA Ops:
  0.6 15.7 %copy-start = (bf16[384,128]{1,0:T(8,128)(2,1)S(1)}, bf16[384,128]{1,0:T(8,128)(2,1)}, u32[]{:S(2)}) copy-start(bf16[384,128]{1,0:T(8,128)(2,1)} %param.18) | copy-start | bytes 294916
  4.6 21.8 %all-to-all-start = ((f32[32,1,5376]{2,1,0:T(1,128)}), f32[32,1,5376]{2,1,0:T(1,128)S(1)}, u32[]{:S(2)}, u32[]{:S(2)}) async-start(f32[32,1,5376]{2,1,0:T(1,128)} %reshape.49), calls=%async_computation | async-start | bytes 1376256 | tf_op jit(solution)/shard_map/all_to_all | solution.py:21
  53.1 33.1 %copy-start.1 = (bf16[32,24,128]{2,1,0:T(8,128)(2,1)S(1)}, bf16[32,24,128]{2,1,0:T(8,128)(2,1)}, u32[]{:S(2)}) copy-start(bf16[32,24,128]{2,1,0:T(8,128)(2,1)} %fusion.12) | copy-start | bytes 589828
  53.1 33.1 %copy-start.3 = (bf16[128,50]{0,1:T(8,128)(2,1)S(1)}, bf16[128,50]{0,1:T(8,128)(2,1)}, u32[]{:S(2)}) copy-start(bf16[128,50]{0,1:T(8,128)(2,1)} %param.22) | copy-start | bytes 38404
  53.1 33.1 %copy-start.4 = (f32[50]{0:T(128)S(1)}, f32[50]{0:T(128)}, u32[]{:S(2)}) copy-start(f32[50]{0:T(128)} %param.23) | copy-start | bytes 604
  53.1 42.8 %copy-start.5 = (f32[50]{0:T(128)S(1)}, f32[50]{0:T(128)}, u32[]{:S(2)}) copy-start(f32[50]{0:T(128)} %add_multiply_fusion) | copy-start | bytes 604
  80.6 13.9 %all-to-all-start.1 = ((f32[32,1,1536]{2,1,0:T(1,128)}), f32[32,1,1536]{2,1,0:T(1,128)S(1)}, u32[]{:S(2)}, u32[]{:S(2)}) async-start(f32[32,1,1536]{2,1,0:T(1,128)} %reshape.51), calls=%async_computation.1 | async-start | bytes 393216 | tf_op jit(solution)/shard_map/all_to_all | solution.py:39
  95.8 37.2 %copy-start.2 = (f32[32,24]{0,1:T(8,128)}, f32[32,24]{0,1:T(8,128)S(1)}, u32[]{:S(2)}) copy-start(f32[32,24]{0,1:T(8,128)S(1)} %fusion.31) | copy-start | bytes 9220
where the time goes:
time: 135 us; the launch traced here: 134 us
  blocking collectives  45.9 us (34%)
  other arithmetic  35 us (26%)
  local copies, waits for them, and re-layouts  17.4 us (13%)
  waiting for transfers between devices  15.4 us (11%)
  starting transfers between devices  14.2 us (11%)
  between operations  3.24 us (2%)
  matrix products  2.91 us (2%)
    psum x4, blocking collectives, over_axes(): shard = lax.psum(shard, axis)  33.9 us
    reduce_sum x1, other arithmetic, local(): preserved = jnp.sum(weights * scores, axis=1)  26.3 us
    all_gather x1, blocking collectives, from_root(): lax.all_gather(shard, axis)  12 us
    all_to_all x1, starting transfers between devices, sent_to_all(): return lax.all_to_all(copies, axis, split_axis=0, concat_axis=0, tiled=True)  8.58 us
    all_to_all x1, waiting for transfers between devices, summed_on_arrival(): parts = lax.all_to_all(split_up(shard, dim, size), axis, 0, 0, tiled=True)  7.99 us
    all_to_all x1, waiting for transfers between devices, sent_to_all(): return lax.all_to_all(copies, axis, split_axis=0, concat_axis=0, tiled=True)  7.45 us
    transpose x2, local copies, waits for them, and re-layouts, in_order(): parts = jnp.moveaxis(parts, 0, dim)  7.29 us
    unnamed x19, local copies, waits for them, and re-layouts  5.59 us
  transfers between devices with their start and end apart: 2, of which 2 were waited for; matrix products, arithmetic and copies ran while one was open for 5% of the time, Pallas kernels for 0%

commit v1 on v0

--- a/solution.py
+++ b/solution.py
@@ -51,7 +51,7 @@
 
 def over_axes(shard, axes):
     for axis in axes:
-        shard = lax.psum(shard, axis)
+        shard = lax.all_gather(shard, axis_name=axis).sum(axis=0)
     return shard
 
 

time: 135 us -> 151 us (1.12)
  local copies, waits for them, and re-layouts: 17.4 us -> 31.8 us
  other arithmetic: 35 us -> 40.2 us
  blocking collectives: 45.9 us -> 43.2 us
    psum x4 -> x0, blocking collectives: 33.9 us -> none  [over_axes(): shard = lax.psum(shard, axis)]
    unnamed x0 -> x4, blocking collectives: none -> 31.2 us
    unnamed x19 -> x45, local copies, waits for them, and re-layouts: 5.59 us -> 19.9 us
    reduce_sum x0 -> x8, other arithmetic: none -> 5.13 us  [over_axes(): shard = lax.all_gather(shard, axis_name=axis).sum(axis=0)]
where the time goes in v1:
time: 151 us; the launch traced here: 150 us
  blocking collectives  43.2 us (29%)
  other arithmetic  40.2 us (27%)
  local copies, waits for them, and re-layouts  31.8 us (21%)
  starting transfers between devices  14.2 us (9%)
  waiting for transfers between devices  14.2 us (9%)
  between operations  3.41 us (2%)
  matrix products  2.91 us (2%)
    unnamed x4, blocking collectives  31.2 us
    reduce_sum x1, other arithmetic, local(): preserved = jnp.sum(weights * scores, axis=1)  26.3 us
    unnamed x45, local copies, waits for them, and re-layouts  19.9 us
    all_gather x1, blocking collectives, from_root(): lax.all_gather(shard, axis)  12 us
    all_to_all x1, starting transfers between devices, sent_to_all(): return lax.all_to_all(copies, axis, split_axis=0, concat_axis=0, tiled=True)  8.58 us
    all_to_all x1, waiting for transfers between devices, summed_on_arrival(): parts = lax.all_to_all(split_up(shard, dim, size), axis, 0, 0, tiled=True)  7.98 us
    transpose x2, local copies, waits for them, and re-layouts, in_order(): parts = jnp.moveaxis(parts, 0, dim)  7.29 us
    all_to_all x1, waiting for transfers between devices, sent_to_all(): return lax.all_to_all(copies, axis, split_axis=0, concat_axis=0, tiled=True)  6.2 us
  transfers between devices with their start and end apart: 2, of which 2 were waited for; matrix products, arithmetic and copies ran while one was open for 5% of the time, Pallas kernels for 0%

profile of v1, /device:TPU:1, one launch (start us, length us, event | category | flops | bytes accessed | tf_op | source)
XLA Modules:
  0.0 149.8 jit_solution(4222566395221166053)
XLA Ops:
  0.6 0.0 copy-start
  0.6 0.8 copy.19
  1.5 0.1 copy.20
  1.5 0.8 pad_maximum_fusion.1
  2.3 0.2 broadcast_bitcast_fusion
  2.5 2.1 %reshape.89 = f32[32,1,5376]{2,1,0:T(1,128)} reshape(f32[32,7,24,32]{3,2,1,0:T(8,128)S(1)} %broadcast_bitcast_fusion) | data formatting | bytes 1376256
  4.6 8.6 %all-to-all-start = ((f32[32,1,5376]{2,1,0:T(1,128)}), f32[32,1,5376]{2,1,0:T(1,128)S(1)}, u32[]{:S(2)}, u32[]{:S(2)}) async-start(f32[32,1,5376]{2,1,0:T(1,128)} %reshape.89), calls=%async_computation | async-start | bytes 1376256 | tf_op jit(solution)/shard_map/all_to_all | solution.py:21
  13.2 1.2 convert_reduce_fusion
  14.4 0.5 add_multiply_fusion
  15.0 1.2 dynamic-slice
  16.2 1.4 fusion.8
  17.6 2.6 %fusion.12 = bf16[32,24,128]{2,1,0:T(8,128)(2,1)} fusion(bf16[32,24,384]{2,1,0:T(8,128)(2,1)} %param.16, f32[384]{0:T(512)} %param.17, f32[32,24]{1,0:T(8,128)S(1)} %add_rsqrt_fusion, f32[32,24]{1,0:T(8,128)S(1)} %broadcast_multiply_fusion, f32[128]{0:T(128)} %param.21, f32[128]{0:T(128)} %param.19, bf16[384,128]{1,0:T(8,128)(2,1)S(1)} %copy-done, ...), kind=kOutput, calls=%fused_computation.19 | convolution fusion | flops 102727680 | bytes 926208 | tf_op jit(solution)/shard_map/dot_general | solution.py:75
  20.2 6.2 %all-to-all-done = f32[32,1,5376]{2,1,0:T(1,128)S(1)} async-done(((f32[32,1,5376]{2,1,0:T(1,128)}), f32[32,1,5376]{2,1,0:T(1,128)S(1)}, u32[]{:S(2)}, u32[]{:S(2)}) %all-to-all-start) | async-done | bytes 688160 | tf_op jit(solution)/shard_map/all_to_all | solution.py:21
  26.4 0.5 broadcast.61
  26.9 2.3 %reduce.8 = f32[32,5376]{1,0:T(8,128)S(1)} reduce(f32[32,1,5376]{2,1,0:T(1,128)S(1)} %all-to-all-done, f32[]{:T(128)} %broadcast.61), dimensions={1}, to_apply=%all_to_all.6.reduce_sub_computation | reduce | bytes 1376260 | tf_op jit(solution)/shard_map/all_to_all | solution.py:21
  29.2 0.8 reshape.90
  30.0 1.7 %bitcast_bitcast_fusion = f32[32,7,32,24]{0,3,1,2:T(8,128)} fusion(f32[32,7,24,32]{3,2,1,0:T(8,128)S(1)} %reshape.90), kind=kLoop, calls=%fused_computation.64 | loop fusion | bytes 1376256 | tf_op jit(solution)/shard_map/transpose | solution.py:14
  31.7 5.6 %copy.21 = f32[32,7,32,24]{3,2,0,1:T(8,128)} copy(f32[32,7,32,24]{0,3,1,2:T(8,128)} %bitcast_bitcast_fusion) | data formatting | bytes 1376256 | tf_op jit(solution)/shard_map/transpose | solution.py:14
  37.3 3.6 %reshape.43 = f32[32,7,768]{2,0,1:T(8,128)S(1)} reshape(f32[32,7,32,24]{3,2,0,1:T(8,128)} %copy.21) | data formatting | bytes 1376256 | tf_op jit(solution)/shard_map/reshape | solution.py:16
  40.9 0.1 constant_dynamic-slice_fusion
  41.0 12.0 %all-gather = f32[128,7,96]{2,0,1:T(8,128)S(1)} all-gather(f32[32,7,96]{2,0,1:T(8,128)S(1)} %constant_dynamic-slice_fusion), channel_id=2, replica_groups=mesh['row'=4,'col_0'=4,'col_1'=4,'col_2'=2] {'row'}, dimensions={0}, use_global_device_ids=true | all-gather | bytes 430080 | tf_op jit(solution)/shard_map/all_gather | solution.py:29
  53.1 0.0 copy-start.1
  53.1 0.0 copy-start.3
  53.1 0.0 copy-start.4
  53.1 0.0 copy-start.8
  53.1 0.0 copy-start.7
  53.1 0.0 copy-start.6
  53.2 0.0 copy-start.5
  53.2 26.3 %multiply_reduce_fusion = (f32[32,768]{1,0:T(8,128)S(1)}, f32[32,768]{1,0:T(8,128)S(1)}) fusion(s32[32,96,768]{2,1,0:T(8,128)} %param.12, f32[32,768]{1,0:T(8,128)S(1)} %get-tuple-element.19, f32[32,96]{1,0:T(8,128)S(1)} %get-tuple-element.26, f32[32,768]{1,0:T(8,128)S(1)} %get-tuple-element.20, f32[32,96]{1,0:T(8,128)S(1)} %get-tuple-element.27, ...), kind=kLoop, calls=%fused_computation.1 | loop fusion | flops 117915648 | bytes 10407936 | tf_op jit(solution)/shard_map/reduce_sum | solution.py:120
  79.5 0.2 copy.22
  79.7 0.9 reshape.91
  80.6 5.6 %all-to-all-start.1 = ((f32[32,1,1536]{2,1,0:T(1,128)}), f32[32,1,1536]{2,1,0:T(1,128)S(1)}, u32[]{:S(2)}, u32[]{:S(2)}) async-start(f32[32,1,1536]{2,1,0:T(1,128)} %reshape.91), calls=%async_computation.1 | async-start | bytes 393216 | tf_op jit(solution)/shard_map/all_to_all | solution.py:39
  86.2 0.3 exponential_reduce_fusion
  86.6 8.0 %all-to-all-done.1 = f32[32,1,1536]{2,1,0:T(1,128)S(1)} async-done(((f32[32,1,1536]{2,1,0:T(1,128)}), f32[32,1,1536]{2,1,0:T(1,128)S(1)}, u32[]{:S(2)}, u32[]{:S(2)}) %all-to-all-start.1) | async-done | bytes 196640 | tf_op jit(solution)/shard_map/all_to_all | solution.py:39
  94.5 1.1 reduce.9
  95.7 0.1 reshape.92
  95.8 0.1 fusion.31
  95.9 0.1 copy.23
  96.0 0.6 fusion.35
  96.6 0.6 fusion.34
  97.2 1.4 dynamic-update-slice
  98.6 1.4 dynamic-update-slice.4
  100.0 0.6 dynamic-slice.1
  100.6 9.0 %all-reduce.10 = (f32[4]{0:T(128)S(1)}, f32[4]{0:T(128)S(1)}) all-reduce(f32[4]{0:T(128)S(1)} %dynamic-update-slice, f32[4]{0:T(128)S(1)} %dynamic-update-slice.4), channel_id=1, replica_groups=mesh['row'=4,'col_0'=4,'col_1'=4,'col_2'=2] {'row'}, use_global_device_ids=true, to_apply=%add | all-reduce | flops 8 | bytes 64
  109.6 0.6 reduce_sum.171
  110.2 0.7 reduce_sum.176
  110.9 1.4 dynamic-update-slice.1
  112.3 1.4 dynamic-update-slice.5
  113.7 0.6 dynamic-slice.2
  114.3 6.8 %all-reduce.9 = (f32[4]{0:T(128)S(1)}, f32[4]{0:T(128)S(1)}) all-reduce(f32[4]{0:T(128)S(1)} %dynamic-update-slice.1, f32[4]{0:T(128)S(1)} %dynamic-update-slice.5), channel_id=1, replica_groups=mesh['row'=4,'col_0'=4,'col_1'=4,'col_2'=2] {'col_0'}, use_global_device_ids=true, to_apply=%add.1 | all-reduce | flops 8 | bytes 64
  121.1 0.6 reduce_sum.172
  121.7 0.7 reduce_sum.177
  122.3 1.4 dynamic-update-slice.2
  123.8 1.4 dynamic-update-slice.6
  125.2 0.6 dynamic-slice.3
  125.8 7.0 %all-reduce.8 = (f32[4]{0:T(128)S(1)}, f32[4]{0:T(128)S(1)}) all-reduce(f32[4]{0:T(128)S(1)} %dynamic-update-slice.2, f32[4]{0:T(128)S(1)} %dynamic-update-slice.6), channel_id=1, replica_groups=mesh['row'=4,'col_0'=4,'col_1'=4,'col_2'=2] {'col_1'}, use_global_device_ids=true, to_apply=%add.2 | all-reduce | flops 8 | bytes 64
  132.8 0.6 reduce_sum.173
  133.4 0.7 reduce_sum.178
  134.1 1.4 dynamic-update-slice.3
  135.5 1.4 dynamic-update-slice.7
  136.9 0.7 copy.24
  137.6 8.5 %all-reduce.11 = (f32[2]{0:T(128)S(1)}, f32[2]{0:T(128)S(1)}) all-reduce(f32[2]{0:T(128)S(1)} %dynamic-update-slice.3, f32[2]{0:T(128)S(1)} %dynamic-update-slice.7), channel_id=1, replica_groups=mesh['row'=4,'col_0'=4,'col_1'=4,'col_2'=2] {'col_2'}, use_global_device_ids=true, to_apply=%add.3 | all-reduce | flops 4 | bytes 32
  146.0 0.6 reduce_sum.174
  146.6 0.7 reduce_sum.179
  (26 shorter events, 0.2 us)
Async XLA Ops:
  0.6 17.0 %copy-start = (bf16[384,128]{1,0:T(8,128)(2,1)S(1)}, bf16[384,128]{1,0:T(8,128)(2,1)}, u32[]{:S(2)}) copy-start(bf16[384,128]{1,0:T(8,128)(2,1)} %param.18) | copy-start | bytes 294916
  4.6 21.8 %all-to-all-start = ((f32[32,1,5376]{2,1,0:T(1,128)}), f32[32,1,5376]{2,1,0:T(1,128)S(1)}, u32[]{:S(2)}, u32[]{:S(2)}) async-start(f32[32,1,5376]{2,1,0:T(1,128)} %reshape.89), calls=%async_computation | async-start | bytes 1376256 | tf_op jit(solution)/shard_map/all_to_all | solution.py:21
  53.1 33.1 %copy-start.1 = (bf16[32,24,128]{2,1,0:T(8,128)(2,1)S(1)}, bf16[32,24,128]{2,1,0:T(8,128)(2,1)}, u32[]{:S(2)}) copy-start(bf16[32,24,128]{2,1,0:T(8,128)(2,1)} %fusion.12) | copy-start | bytes 589828
  53.1 33.1 %copy-start.3 = (bf16[128,50]{0,1:T(8,128)(2,1)S(1)}, bf16[128,50]{0,1:T(8,128)(2,1)}, u32[]{:S(2)}) copy-start(bf16[128,50]{0,1:T(8,128)(2,1)} %param.22) | copy-start | bytes 38404
  53.1 33.1 %copy-start.4 = (f32[50]{0:T(128)S(1)}, f32[50]{0:T(128)}, u32[]{:S(2)}) copy-start(f32[50]{0:T(128)} %param.23) | copy-start | bytes 604
  53.1 42.9 %copy-start.8 = (f32[50]{0:T(128)S(1)}, f32[50]{0:T(128)}, u32[]{:S(2)}) copy-start(f32[50]{0:T(128)} %add_multiply_fusion) | copy-start | bytes 604
  53.1 46.9 %copy-start.7 = (u32[128]{0:T(128)S(1)}, u32[128]{0:T(128)}, u32[]{:S(2)}) copy-start(u32[128]{0:T(128)} %constant.82) | copy-start | bytes 1540
  53.1 60.6 %copy-start.6 = (u32[128]{0:T(128)S(1)}, u32[128]{0:T(128)}, u32[]{:S(2)}) copy-start(u32[128]{0:T(128)} %constant.87) | copy-start | bytes 1540
  53.2 72.0 %copy-start.5 = (u32[128]{0:T(128)S(1)}, u32[128]{0:T(128)}, u32[]{:S(2)}) copy-start(u32[128]{0:T(128)} %constant.92) | copy-start | bytes 1540
  80.6 13.9 %all-to-all-start.1 = ((f32[32,1,1536]{2,1,0:T(1,128)}), f32[32,1,1536]{2,1,0:T(1,128)S(1)}, u32[]{:S(2)}, u32[]{:S(2)}) async-start(f32[32,1,1536]{2,1,0:T(1,128)} %reshape.91), calls=%async_computation.1 | async-start | bytes 393216 | tf_op jit(solution)/shard_map/all_to_all | solution.py:39
  95.9 52.8 %copy-start.2 = (f32[32,24]{0,1:T(8,128)}, f32[32,24]{0,1:T(8,128)S(1)}, u32[]{:S(2)}) copy-start(f32[32,24]{0,1:T(8,128)S(1)} %fusion.31) | copy-start | bytes 9220
